TPU v7x, 32 devices: a whole 2x2x4 slice. The times are simulated.
32 devices in a mesh: grp: 2 (over y), row: 8 (over z, x), col: 1, ch: 2 (over core).
Axes of the slice: x: 2, y: 2, z: 4, core: 2. Of those that a mesh axis runs over, the one named last changes fastest.
Arguments:
- pair_act: bfloat16 [128, 256, 128], P('ch', ('grp', 'row'), 'col'), parts along dimension 1, may hold values from -48 to 48
- in_gain: float32 [128], P('ch'), may hold values from 0.1 to 1.9
- left_proj: bfloat16 [128, 128], P(None, 'ch'), may hold values from -0.5 to 0.5
- left_gate: bfloat16 [128, 128], P(None, 'ch'), may hold values from -0.5 to 0.5
- right_proj: bfloat16 [128, 128], P(None, 'ch'), may hold values from -0.5 to 0.5
- right_gate: bfloat16 [128, 128], P(None, 'ch'), may hold values from -0.5 to 0.5
- out_gate: bfloat16 [128, 128], P(None, 'ch'), may hold values from -0.5 to 0.5
- out_gain: float32 [128], P('ch'), may hold values from 0.1 to 1.9
- out_proj: bfloat16 [128, 128], P(None, 'ch'), may hold values from -0.5 to 0.5
Outputs:
- update: bfloat16 [128, 256, 128], P('ch', ('grp', 'row'), 'col'), parts along dimension 1
There are 2 independent parts, one for each index of `grp`. A program takes and returns all parts, laid end to end along the dimension named above; an argument that names none is the same for every part. Nothing has to cross between parts.
All inputs are finite; a program needn't handle non-finite values.
Results may differ from a plain program's by a relative error of at most 0.0085.
Values may be sent and summed in bfloat16 or wider, within the bound.
No kernel may reach another device: no remote copies, remote signals or barrier semaphores. Data moves between devices by JAX's collectives and lax.ppermute only.
A program may use at most 64 MiB of HBM per device.

v0:
```python
import functools

import jax
import jax.numpy as jnp
from jax import lax
from jax.experimental import pallas as pl
from jax.experimental.pallas import tpu as pltpu
from jax.sharding import PartitionSpec as P


F32 = jnp.float32
BF16 = jnp.bfloat16
EPS = 1e-05


def near(value):
    return pltpu.with_memory_space_constraint(value, pltpu.VMEM)


def call(body, out_shapes, scratch, flops, *operands):
    return pl.pallas_call(
        body,
        out_shape=out_shapes,
        scratch_shapes=scratch,
        in_specs=[pl.BlockSpec(memory_space=pltpu.VMEM)] * len(operands),
        out_specs=jax.tree.map(lambda _: pl.BlockSpec(memory_space=pltpu.VMEM), out_shapes),
        cost_estimate=pl.CostEstimate(flops=flops, bytes_accessed=1 << 20, transcendentals=0),
    )(*operands)


def channel_parts(value):
    count = lax.axis_size("ch")
    return [value] + [
        near(lax.ppermute(value, "ch", [((i + s) % count, i) for i in range(count)]))
        for s in range(1, count)
    ]


def row_exchange(blocks):
    count = lax.axis_size("row")
    arrived = [blocks[0]]
    for d in range(1, count):
        arrived.append(lax.ppermute(blocks[d], "row", [(i, i ^ d) for i in range(count)]))
    return arrived


def part_start(s, count, size):
    return pl.multiple_of(((lax.axis_index("ch") + s) % count) * size, size)


def fill_gains(gains, gain_scr):
    count = len(gains)
    size = gains[0].shape[0]
    lanes = gain_scr.shape[1]
    for s in range(count):
        line = jnp.broadcast_to(gains[s][...].reshape(1, size), (lanes, size))
        gain_scr[pl.ds(part_start(s, count, size), size), :] = line.T


def normalise(values, gain):
    average = jnp.mean(values, axis=0, keepdims=True)
    centred = values - average
    spread = jnp.mean(centred * centred, axis=0, keepdims=True)
    return (centred * lax.rsqrt(spread + EPS) * gain).astype(BF16)


def edges_body(count, row_count, *refs):
    acts, gains = refs[:count], refs[count : 2 * count]
    lp, lg, rp, rg = refs[2 * count : 2 * count + 4]
    outs = refs[2 * count + 4 : 2 * count + 4 + row_count]
    normed_ref, flat, gain_scr, weights = refs[2 * count + 4 + row_count :]
    size, rows, cols = acts[0].shape
    channels = size * count
    hidden = lp.shape[0]
    group = hidden // row_count
    me = lax.axis_index("row")
    fill_gains(gains, gain_scr)
    for s in range(count):
        flat[pl.ds(part_start(s, count, size) * rows, size * rows), :] = (
            acts[s][...].astype(F32).reshape(size * rows, cols)
        )
    for n, w in enumerate((lp, rp, lg, rg)):
        weights[n] = w[...].astype(F32)
    pieces = []
    for pair in ((0, 1), (2, 3)):
        for d in range(row_count):
            start = pl.multiple_of((me ^ d) * group, group)
            for n in pair:
                pieces.append(weights[n, pl.ds(start, group), :])
    stacked = jnp.concatenate(pieces, axis=0).astype(BF16)
    half = 2 * hidden
    gain = gain_scr[...]
    for x in range(rows):
        normed = normalise(flat[pl.ds(x, channels, stride=rows), :], gain)
        normed_ref[x] = normed
        lifted = jnp.dot(stacked, normed, preferred_element_type=F32)
        edges = (jax.nn.sigmoid(lifted[half:]) * lifted[:half]).astype(BF16)
        for d in range(row_count):
            outs[d][x] = edges[2 * group * d : 2 * group * (d + 1)]


def gate_body(normed, weight, out):
    for x in range(normed.shape[0]):
        out[x] = jax.nn.sigmoid(jnp.dot(weight[...], normed[x], preferred_element_type=F32))


def triangle_body(row_count, separate, *refs):
    blocks = refs[:row_count]
    refs = refs[row_count:]
    if separate:
        left_ref, refs = refs[0], refs[1:]
    outs, refs = refs[:row_count], refs[row_count:]
    flat, tri = refs[:2]
    rows, pair, cols = blocks[0].shape
    group = pair // 2
    depth = rows * row_count
    me = lax.axis_index("row")
    for d in range(row_count):
        flat[pl.ds(d * rows * pair, rows * pair), :] = (
            blocks[d][...].astype(F32).reshape(rows * pair, cols)
        )
    for h in range(group):
        right = flat[pl.ds(group + h, depth, stride=pair), :].astype(BF16)
        if separate:
            left = left_ref[h]
        else:
            left = flat[pl.ds(h, depth, stride=pair), :].astype(BF16)
        tri[h] = lax.dot_general(
            left, right, (((0,), (0,)), ((), ())), preferred_element_type=F32
        )
    for d in range(row_count):
        start = pl.multiple_of((me ^ d) * rows, rows)
        outs[d][...] = tri[:, pl.ds(start, rows), :].astype(BF16)


def update_body(count, row_count, *refs):
    tris, gains = refs[:count], refs[count : 2 * count]
    gate, weight, out, flat, gain_scr, wide = refs[2 * count :]
    size, rows, cols = tris[0].shape
    group = size // row_count
    channels = size * count
    me = lax.axis_index("row")
    fill_gains(gains, gain_scr)
    for s in range(count):
        base = part_start(s, count, size)
        for d in range(row_count):
            start = pl.multiple_of((base + (me ^ d) * group) * rows, group * rows)
            flat[pl.ds(start, group * rows), :] = (
                tris[s][group * d : group * (d + 1)].astype(F32).reshape(group * rows, cols)
            )
    gain = gain_scr[...]
    outs = weight.shape[0]
    for x in range(rows):
        mid = normalise(flat[pl.ds(x, channels, stride=rows), :], gain)
        projected = jnp.dot(weight[...], mid, preferred_element_type=F32)
        wide[pl.ds(x, outs, stride=rows), :] = gate[x] * projected
    out[...] = wide[...].reshape(outs, rows, cols).astype(BF16)


def steps(
    pair_act, in_gain, left_proj, left_gate, right_proj, right_gate, out_gate, out_gain, out_proj
):
    size, rows, cols = pair_act.shape
    count = lax.axis_size("ch")
    row_count = lax.axis_size("row")
    col_count = lax.axis_size("col")
    channels = size * count
    hidden = left_proj.shape[1]
    hidden_all = hidden * count
    group = hidden // row_count
    outs = out_proj.shape[1]
    shape = pltpu.VMEM

    acts = channel_parts(pair_act)
    in_gains = channel_parts(in_gain)
    out_gains = channel_parts(out_gain)
    *edges, normed = call(
        functools.partial(edges_body, count, row_count),
        [shape((rows, 2 * group, cols), BF16)] * row_count + [shape((rows, channels, cols), BF16)],
        [
            pltpu.VMEM((channels * rows, cols), F32),
            pltpu.VMEM((channels, cols), F32),
            pltpu.VMEM((4, hidden, channels), F32),
        ],
        8 * hidden * channels * rows * cols,
        *acts, *in_gains, left_proj.T, left_gate.T, right_proj.T, right_gate.T,
    )
    arrived = row_exchange(edges)
    gate_map = call(
        gate_body, shape((rows, outs, cols), F32), [], 2 * outs * channels * rows * cols,
        near(normed), out_gate.T,
    )
    depth = rows * row_count
    separate = col_count > 1
    extra = ()
    if separate:
        left = jnp.concatenate(arrived, axis=0)[:, :group].transpose(1, 0, 2)
        extra = (lax.all_gather(left, "col", axis=2, tiled=True),)
    tri_blocks = call(
        functools.partial(triangle_body, row_count, separate),
        [shape((group, rows, cols), BF16)] * row_count,
        [
            pltpu.VMEM((depth * 2 * group, cols), F32),
            pltpu.VMEM((group, cols * col_count, cols), F32),
        ],
        2 * group * depth * cols * cols * col_count,
        *map(near, arrived), *extra,
    )
    tri = jnp.concatenate(row_exchange(tri_blocks), axis=0)
    tris = channel_parts(tri)
    return call(
        functools.partial(update_body, count, row_count),
        jax.ShapeDtypeStruct((outs, rows, cols), BF16),
        [
            pltpu.VMEM((hidden_all * rows, cols), F32),
            pltpu.VMEM((hidden_all, cols), F32),
            pltpu.VMEM((outs * rows, cols), F32),
        ],
        2 * hidden_all * outs * rows * cols,
        near(tri), *tris[1:], *out_gains, near(gate_map), out_proj.T,
    )


def solution(mesh):
    return jax.shard_map(
        steps,
        mesh=mesh,
        in_specs=(
            P("ch", ("grp", "row"), "col"),
            P("ch"),
            P(None, "ch"),
            P(None, "ch"),
            P(None, "ch"),
            P(None, "ch"),
            P(None, "ch"),
            P("ch"),
            P(None, "ch"),
        ),
        out_specs=P("ch", ("grp", "row"), "col"),
        check_vma=False,
    )
```

profile of v0, /device:TPU:0, one launch (start us, length us, event | category | flops | bytes accessed | tf_op | source)
XLA Modules:
  0.0 43.4 jit_solution(18180753944375757369)
XLA Ops:
  0.0 0.5 %collective-permute-start = (bf16[64,16,128]{2,1,0:T(8,128)(2,1)}, bf16[64,16,128]{2,1,0:T(8,128)(2,1)S(1)}, u32[]{:S(2)}, u32[]{:S(2)}) collective-permute-start(bf16[64,16,128]{2,1,0:T(8,128)(2,1)} %refs_0_.1), channel_id=1, source_target_pairs={{1,0},{0,1},{3,2},{2,3},{5,4},{4,5},{7,6},{6,7},{9,8},{8,9},{11,10... | collective-permute-start | bytes 786440 | tf_op jit(solution)/shard_map/ppermute | solution.py:34
  0.5 1.4 %collective-permute-done.1.refs_3_ = f32[64]{0:T(128)S(1)} collective-permute-done((f32[64]{0:T(128)}, f32[64]{0:T(128)S(1)}, u32[]{:S(2)}, u32[]{:S(2)}) %collective-permute-start.1) | collective-permute-done | bytes 288 | tf_op jit(solution)/shard_map/ppermute | solution.py:34
  1.9 2.0 %shard_map.91 = (bf16[16,16,128]{2,1,0:T(8,128)(2,1)S(1)}, bf16[16,16,128]{2,1,0:T(8,128)(2,1)S(1)}, bf16[16,16,128]{2,1,0:T(8,128)(2,1)S(1)}, bf16[16,16,128]{2...) custom-call(bf16[64,16,128]{2,1,0:T(8,128)(2,1)} %refs_0_.1, ...), custom_call_target="tpu_custom_call" | custom-call | flops 134217728 | bytes 1048576 | tf_op jit(solution)/shard_map/pallas_call | solution.py:21
  3.9 2.9 %collective-permute-start.2 = (bf16[16,16,128]{2,1,0:T(8,128)(2,1)S(1)}, bf16[16,16,128]{2,1,0:T(8,128)(2,1)S(1)}, u32[]{:S(2)}, u32[]{:S(2)}) collective-permute-start(bf16[16,16,128]{2,1,0:T(8,128)(2,1)S(1)} %get-tuple-element.23), channel_id=1, source_target_pairs={{0,2},{2,0},{4,6},{6,4},{8,10},{10,8},{12,14},{14,12},{1,3},{3,1},... | collective-permute-start | bytes 196616 | tf_op jit(solution)/shard_map/ppermute | solution.py:43
  6.8 1.6 %collective-permute-start.3 = (bf16[16,16,128]{2,1,0:T(8,128)(2,1)S(1)}, bf16[16,16,128]{2,1,0:T(8,128)(2,1)S(1)}, u32[]{:S(2)}, u32[]{:S(2)}) collective-permute-start(bf16[16,16,128]{2,1,0:T(8,128)(2,1)S(1)} %get-tuple-element.24), channel_id=1, source_target_pairs={{0,4},{2,6},{4,0},{6,2},{8,12},{10,14},{12,8},{14,10},{1,5},{3,7},... | collective-permute-start | bytes 196616 | tf_op jit(solution)/shard_map/ppermute | solution.py:43
  8.4 3.0 %collective-permute-start.5 = (bf16[16,16,128]{2,1,0:T(8,128)(2,1)S(1)}, bf16[16,16,128]{2,1,0:T(8,128)(2,1)S(1)}, u32[]{:S(2)}, u32[]{:S(2)}) collective-permute-start(bf16[16,16,128]{2,1,0:T(8,128)(2,1)S(1)} %get-tuple-element.26), channel_id=1, source_target_pairs={{0,8},{2,10},{4,12},{6,14},{8,0},{10,2},{12,4},{14,6},{1,9},{3,11}... | collective-permute-start | bytes 196616 | tf_op jit(solution)/shard_map/ppermute | solution.py:43
  11.4 1.3 %collective-permute-start.6 = (bf16[16,16,128]{2,1,0:T(8,128)(2,1)S(1)}, bf16[16,16,128]{2,1,0:T(8,128)(2,1)S(1)}, u32[]{:S(2)}, u32[]{:S(2)}) collective-permute-start(bf16[16,16,128]{2,1,0:T(8,128)(2,1)S(1)} %get-tuple-element.27), channel_id=1, source_target_pairs={{0,10},{2,8},{4,14},{6,12},{8,2},{10,0},{12,6},{14,4},{1,11},{3,9}... | collective-permute-start | bytes 196616 | tf_op jit(solution)/shard_map/ppermute | solution.py:43
  12.7 3.6 %collective-permute-start.7 = (bf16[16,16,128]{2,1,0:T(8,128)(2,1)S(1)}, bf16[16,16,128]{2,1,0:T(8,128)(2,1)S(1)}, u32[]{:S(2)}, u32[]{:S(2)}) collective-permute-start(bf16[16,16,128]{2,1,0:T(8,128)(2,1)S(1)} %get-tuple-element.28), channel_id=1, source_target_pairs={{0,12},{2,14},{4,8},{6,10},{8,4},{10,6},{12,0},{14,2},{1,13},{3,15... | collective-permute-start | bytes 196616 | tf_op jit(solution)/shard_map/ppermute | solution.py:43
  16.3 5.5 %collective-permute-done.6.refs_5_ = bf16[16,16,128]{2,1,0:T(8,128)(2,1)S(1)} collective-permute-done((bf16[16,16,128]{2,1,0:T(8,128)(2,1)S(1)}, bf16[16,16,128]{2,1,0:T(8,128)(2,1)S(1)}, u32[]{:S(2)}, u32[]{:S(2)}) %collective-permute-start.6) | collective-permute-done | bytes 65568 | tf_op jit(solution)/shard_map/ppermute | solution.py:43
  21.9 1.5 %collective-permute-done.8.refs_7_ = bf16[16,16,128]{2,1,0:T(8,128)(2,1)S(1)} collective-permute-done((bf16[16,16,128]{2,1,0:T(8,128)(2,1)S(1)}, bf16[16,16,128]{2,1,0:T(8,128)(2,1)S(1)}, u32[]{:S(2)}, u32[]{:S(2)}) %collective-permute-start.8) | collective-permute-done | bytes 65568 | tf_op jit(solution)/shard_map/ppermute | solution.py:43
  23.3 0.5 %shard_map.92 = (bf16[8,16,128]{2,1,0:T(8,128)(2,1)S(1)}, bf16[8,16,128]{2,1,0:T(8,128)(2,1)S(1)}, bf16[8,16,128]{2,1,0:T(8,128)(2,1)S(1)}, bf16[8,16,128]{2,1,0...) custom-call(bf16[16,16,128]{2,1,0:T(8,128)(2,1)S(1)} %get-tuple-elem, ...), custom_call_target="tpu_custom_call" | custom-call | flops 33554432 | bytes 1048576 | tf_op jit(solution)/shard_map/pallas_call | solution.py:21
  23.9 0.6 %collective-permute-start.9 = (bf16[8,16,128]{2,1,0:T(8,128)(2,1)S(1)}, bf16[8,16,128]{2,1,0:T(8,128)(2,1)S(1)}, u32[]{:S(2)}, u32[]{:S(2)}) collective-permute-start(bf16[8,16,128]{2,1,0:T(8,128)(2,1)S(1)} %get-tuple-element.31), channel_id=1, source_target_pairs={{0,2},{2,0},{4,6},{6,4},{8,10},{10,8},{12,14},{14,12},{1,3},{3,1},... | collective-permute-start | bytes 98312 | tf_op jit(solution)/shard_map/ppermute | solution.py:43
  24.5 2.2 %collective-permute-start.10 = (bf16[8,16,128]{2,1,0:T(8,128)(2,1)S(1)}, bf16[8,16,128]{2,1,0:T(8,128)(2,1)S(1)}, u32[]{:S(2)}, u32[]{:S(2)}) collective-permute-start(bf16[8,16,128]{2,1,0:T(8,128)(2,1)S(1)} %get-tuple-element.32), channel_id=1, source_target_pairs={{0,4},{2,6},{4,0},{6,2},{8,12},{10,14},{12,8},{14,10},{1,5},{3,7},... | collective-permute-start | bytes 98312 | tf_op jit(solution)/shard_map/ppermute | solution.py:43
  26.7 0.7 %collective-permute-start.11 = (bf16[8,16,128]{2,1,0:T(8,128)(2,1)S(1)}, bf16[8,16,128]{2,1,0:T(8,128)(2,1)S(1)}, u32[]{:S(2)}, u32[]{:S(2)}) collective-permute-start(bf16[8,16,128]{2,1,0:T(8,128)(2,1)S(1)} %get-tuple-element.33), channel_id=1, source_target_pairs={{0,6},{2,4},{4,2},{6,0},{8,14},{10,12},{12,10},{14,8},{1,7},{3,5},... | collective-permute-start | bytes 98312 | tf_op jit(solution)/shard_map/ppermute | solution.py:43
  27.5 3.0 %collective-permute-start.12 = (bf16[8,16,128]{2,1,0:T(8,128)(2,1)S(1)}, bf16[8,16,128]{2,1,0:T(8,128)(2,1)S(1)}, u32[]{:S(2)}, u32[]{:S(2)}) collective-permute-start(bf16[8,16,128]{2,1,0:T(8,128)(2,1)S(1)} %get-tuple-element.34), channel_id=1, source_target_pairs={{0,8},{2,10},{4,12},{6,14},{8,0},{10,2},{12,4},{14,6},{1,9},{3,11}... | collective-permute-start | bytes 98312 | tf_op jit(solution)/shard_map/ppermute | solution.py:43
  30.5 0.1 collective-permute-start.13
  30.6 2.3 %collective-permute-start.14 = (bf16[8,16,128]{2,1,0:T(8,128)(2,1)S(1)}, bf16[8,16,128]{2,1,0:T(8,128)(2,1)S(1)}, u32[]{:S(2)}, u32[]{:S(2)}) collective-permute-start(bf16[8,16,128]{2,1,0:T(8,128)(2,1)S(1)} %get-tuple-element.36), channel_id=1, source_target_pairs={{0,12},{2,14},{4,8},{6,10},{8,4},{10,6},{12,0},{14,2},{1,13},{3,15... | collective-permute-start | bytes 98312 | tf_op jit(solution)/shard_map/ppermute | solution.py:43
  32.9 2.4 %collective-permute-start.15 = (bf16[8,16,128]{2,1,0:T(8,128)(2,1)S(1)}, bf16[8,16,128]{2,1,0:T(8,128)(2,1)S(1)}, u32[]{:S(2)}, u32[]{:S(2)}) collective-permute-start(bf16[8,16,128]{2,1,0:T(8,128)(2,1)S(1)} %get-tuple-element.37), channel_id=1, source_target_pairs={{0,14},{2,12},{4,10},{6,8},{8,6},{10,4},{12,2},{14,0},{1,15},{3,13... | collective-permute-start | bytes 98312 | tf_op jit(solution)/shard_map/ppermute | solution.py:43
  35.3 0.9 %collective-permute-done.13 = bf16[8,16,128]{2,1,0:T(8,128)(2,1)S(1)} collective-permute-done((bf16[8,16,128]{2,1,0:T(8,128)(2,1)S(1)}, bf16[8,16,128]{2,1,0:T(8,128)(2,1)S(1)}, u32[]{:S(2)}, u32[]{:S(2)}) %collective-permute-start.13) | collective-permute-done | bytes 32800 | tf_op jit(solution)/shard_map/ppermute | solution.py:43
  36.2 0.2 collective-permute-done.14
  36.4 3.2 %collective-permute-done.15 = bf16[8,16,128]{2,1,0:T(8,128)(2,1)S(1)} collective-permute-done((bf16[8,16,128]{2,1,0:T(8,128)(2,1)S(1)}, bf16[8,16,128]{2,1,0:T(8,128)(2,1)S(1)}, u32[]{:S(2)}, u32[]{:S(2)}) %collective-permute-start.15) | collective-permute-done | bytes 32800 | tf_op jit(solution)/shard_map/ppermute | solution.py:43
  39.6 0.5 %collective-permute-start.17 = (f32[64]{0:T(128)S(1)}, f32[64]{0:T(128)S(1)}, u32[]{:S(2)}, u32[]{:S(2)}) collective-permute-start(f32[64]{0:T(128)S(1)} %copy-done), channel_id=1, source_target_pairs={{1,0},{0,1},{3,2},{2,3},{5,4},{4,5},{7,6},{6,7},{9,8},{8,9},{11,10... | collective-permute-start | bytes 776 | tf_op jit(solution)/shard_map/ppermute | solution.py:34
  40.1 1.0 %shard_map.93.refs_4_ = f32[16,64,128]{2,1,0:T(8,128)S(1)} custom-call(bf16[16,128,128]{2,1,0:T(8,128)(2,1)S(1)} %get-tuple-element.38.normed, bf16[64,128]{1,0:T(8,128)(2,1)} %bitcast.6), custom_call_target="tpu_custom_call" | custom-call | flops 33554432 | bytes 1048576 | tf_op jit(solution)/shard_map/pallas_call | solution.py:21
  41.1 2.4 %shard_map.94 = bf16[64,16,128]{2,1,0:T(8,128)(2,1)} custom-call(bf16[64,16,128]{2,1,0:T(8,128)(2,1)S(1)} %constant_dynamic-update-slice_fusion.refs_0_, bf16[64,16,128]{2,1,0:T(8,128)(2,1)S(1)} %collective-permute-done.16.refs_1_, f32[64]{0:T(128)} %refs_2_.3, f32[64]{0:T(128)S(1)} %collective-permute-done.17.refs_3_, ...), custom_call_target="tpu_custom_call" | custom-call | flops 33554432 | bytes 1048576 | tf_op jit(solution)/shard_map/pallas_call | solution.py:21
  (26 shorter events, 0.2 us)
Async XLA Ops:
  0.0 1.9 %collective-permute-start = (bf16[64,16,128]{2,1,0:T(8,128)(2,1)}, bf16[64,16,128]{2,1,0:T(8,128)(2,1)S(1)}, u32[]{:S(2)}, u32[]{:S(2)}) collective-permute-start(bf16[64,16,128]{2,1,0:T(8,128)(2,1)} %refs_0_.1), channel_id=1, source_target_pairs={{1,0},{0,1},{3,2},{2,3},{5,4},{4,5},{7,6},{6,7},{9,8},{8,9},{11,10... | collective-permute-start | bytes 786440 | tf_op jit(solution)/shard_map/ppermute | solution.py:34
  0.5 1.4 %collective-permute-start.1 = (f32[64]{0:T(128)}, f32[64]{0:T(128)S(1)}, u32[]{:S(2)}, u32[]{:S(2)}) collective-permute-start(f32[64]{0:T(128)} %refs_2_.2), channel_id=1, source_target_pairs={{1,0},{0,1},{3,2},{2,3},{5,4},{4,5},{7,6},{6,7},{9,8},{8,9},{11,10... | collective-permute-start | bytes 776 | tf_op jit(solution)/shard_map/ppermute | solution.py:34
  3.9 8.8 %collective-permute-start.2 = (bf16[16,16,128]{2,1,0:T(8,128)(2,1)S(1)}, bf16[16,16,128]{2,1,0:T(8,128)(2,1)S(1)}, u32[]{:S(2)}, u32[]{:S(2)}) collective-permute-start(bf16[16,16,128]{2,1,0:T(8,128)(2,1)S(1)} %get-tuple-element.23), channel_id=1, source_target_pairs={{0,2},{2,0},{4,6},{6,4},{8,10},{10,8},{12,14},{14,12},{1,3},{3,1},... | collective-permute-start | bytes 196616 | tf_op jit(solution)/shard_map/ppermute | solution.py:43
  6.8 9.5 %collective-permute-start.3 = (bf16[16,16,128]{2,1,0:T(8,128)(2,1)S(1)}, bf16[16,16,128]{2,1,0:T(8,128)(2,1)S(1)}, u32[]{:S(2)}, u32[]{:S(2)}) collective-permute-start(bf16[16,16,128]{2,1,0:T(8,128)(2,1)S(1)} %get-tuple-element.24), channel_id=1, source_target_pairs={{0,4},{2,6},{4,0},{6,2},{8,12},{10,14},{12,8},{14,10},{1,5},{3,7},... | collective-permute-start | bytes 196616 | tf_op jit(solution)/shard_map/ppermute | solution.py:43
  8.4 7.9 %collective-permute-start.4 = (bf16[16,16,128]{2,1,0:T(8,128)(2,1)S(1)}, bf16[16,16,128]{2,1,0:T(8,128)(2,1)S(1)}, u32[]{:S(2)}, u32[]{:S(2)}) collective-permute-start(bf16[16,16,128]{2,1,0:T(8,128)(2,1)S(1)} %get-tuple-element.25), channel_id=1, source_target_pairs={{0,6},{2,4},{4,2},{6,0},{8,14},{10,12},{12,10},{14,8},{1,7},{3,5},... | collective-permute-start | bytes 196616 | tf_op jit(solution)/shard_map/ppermute | solution.py:43
  8.4 7.9 %collective-permute-start.5 = (bf16[16,16,128]{2,1,0:T(8,128)(2,1)S(1)}, bf16[16,16,128]{2,1,0:T(8,128)(2,1)S(1)}, u32[]{:S(2)}, u32[]{:S(2)}) collective-permute-start(bf16[16,16,128]{2,1,0:T(8,128)(2,1)S(1)} %get-tuple-element.26), channel_id=1, source_target_pairs={{0,8},{2,10},{4,12},{6,14},{8,0},{10,2},{12,4},{14,6},{1,9},{3,11}... | collective-permute-start | bytes 196616 | tf_op jit(solution)/shard_map/ppermute | solution.py:43
  11.4 10.5 %collective-permute-start.6 = (bf16[16,16,128]{2,1,0:T(8,128)(2,1)S(1)}, bf16[16,16,128]{2,1,0:T(8,128)(2,1)S(1)}, u32[]{:S(2)}, u32[]{:S(2)}) collective-permute-start(bf16[16,16,128]{2,1,0:T(8,128)(2,1)S(1)} %get-tuple-element.27), channel_id=1, source_target_pairs={{0,10},{2,8},{4,14},{6,12},{8,2},{10,0},{12,6},{14,4},{1,11},{3,9}... | collective-permute-start | bytes 196616 | tf_op jit(solution)/shard_map/ppermute | solution.py:43
  12.7 9.2 %collective-permute-start.7 = (bf16[16,16,128]{2,1,0:T(8,128)(2,1)S(1)}, bf16[16,16,128]{2,1,0:T(8,128)(2,1)S(1)}, u32[]{:S(2)}, u32[]{:S(2)}) collective-permute-start(bf16[16,16,128]{2,1,0:T(8,128)(2,1)S(1)} %get-tuple-element.28), channel_id=1, source_target_pairs={{0,12},{2,14},{4,8},{6,10},{8,4},{10,6},{12,0},{14,2},{1,13},{3,15... | collective-permute-start | bytes 196616 | tf_op jit(solution)/shard_map/ppermute | solution.py:43
  16.3 7.1 %collective-permute-start.8 = (bf16[16,16,128]{2,1,0:T(8,128)(2,1)S(1)}, bf16[16,16,128]{2,1,0:T(8,128)(2,1)S(1)}, u32[]{:S(2)}, u32[]{:S(2)}) collective-permute-start(bf16[16,16,128]{2,1,0:T(8,128)(2,1)S(1)} %get-tuple-element.29), channel_id=1, source_target_pairs={{0,14},{2,12},{4,10},{6,8},{8,6},{10,4},{12,2},{14,0},{1,15},{3,13... | collective-permute-start | bytes 196616 | tf_op jit(solution)/shard_map/ppermute | solution.py:43
  23.9 6.7 %collective-permute-start.9 = (bf16[8,16,128]{2,1,0:T(8,128)(2,1)S(1)}, bf16[8,16,128]{2,1,0:T(8,128)(2,1)S(1)}, u32[]{:S(2)}, u32[]{:S(2)}) collective-permute-start(bf16[8,16,128]{2,1,0:T(8,128)(2,1)S(1)} %get-tuple-element.31), channel_id=1, source_target_pairs={{0,2},{2,0},{4,6},{6,4},{8,10},{10,8},{12,14},{14,12},{1,3},{3,1},... | collective-permute-start | bytes 98312 | tf_op jit(solution)/shard_map/ppermute | solution.py:43
  24.5 8.4 %collective-permute-start.10 = (bf16[8,16,128]{2,1,0:T(8,128)(2,1)S(1)}, bf16[8,16,128]{2,1,0:T(8,128)(2,1)S(1)}, u32[]{:S(2)}, u32[]{:S(2)}) collective-permute-start(bf16[8,16,128]{2,1,0:T(8,128)(2,1)S(1)} %get-tuple-element.32), channel_id=1, source_target_pairs={{0,4},{2,6},{4,0},{6,2},{8,12},{10,14},{12,8},{14,10},{1,5},{3,7},... | collective-permute-start | bytes 98312 | tf_op jit(solution)/shard_map/ppermute | solution.py:43
  26.7 8.6 %collective-permute-start.11 = (bf16[8,16,128]{2,1,0:T(8,128)(2,1)S(1)}, bf16[8,16,128]{2,1,0:T(8,128)(2,1)S(1)}, u32[]{:S(2)}, u32[]{:S(2)}) collective-permute-start(bf16[8,16,128]{2,1,0:T(8,128)(2,1)S(1)} %get-tuple-element.33), channel_id=1, source_target_pairs={{0,6},{2,4},{4,2},{6,0},{8,14},{10,12},{12,10},{14,8},{1,7},{3,5},... | collective-permute-start | bytes 98312 | tf_op jit(solution)/shard_map/ppermute | solution.py:43
  27.5 7.9 %collective-permute-start.12 = (bf16[8,16,128]{2,1,0:T(8,128)(2,1)S(1)}, bf16[8,16,128]{2,1,0:T(8,128)(2,1)S(1)}, u32[]{:S(2)}, u32[]{:S(2)}) collective-permute-start(bf16[8,16,128]{2,1,0:T(8,128)(2,1)S(1)} %get-tuple-element.34), channel_id=1, source_target_pairs={{0,8},{2,10},{4,12},{6,14},{8,0},{10,2},{12,4},{14,6},{1,9},{3,11}... | collective-permute-start | bytes 98312 | tf_op jit(solution)/shard_map/ppermute | solution.py:43
  30.5 5.7 %collective-permute-start.13 = (bf16[8,16,128]{2,1,0:T(8,128)(2,1)S(1)}, bf16[8,16,128]{2,1,0:T(8,128)(2,1)S(1)}, u32[]{:S(2)}, u32[]{:S(2)}) collective-permute-start(bf16[8,16,128]{2,1,0:T(8,128)(2,1)S(1)} %get-tuple-element.35), channel_id=1, source_target_pairs={{0,10},{2,8},{4,14},{6,12},{8,2},{10,0},{12,6},{14,4},{1,11},{3,9}... | collective-permute-start | bytes 98312 | tf_op jit(solution)/shard_map/ppermute | solution.py:43
  30.6 5.8 %collective-permute-start.14 = (bf16[8,16,128]{2,1,0:T(8,128)(2,1)S(1)}, bf16[8,16,128]{2,1,0:T(8,128)(2,1)S(1)}, u32[]{:S(2)}, u32[]{:S(2)}) collective-permute-start(bf16[8,16,128]{2,1,0:T(8,128)(2,1)S(1)} %get-tuple-element.36), channel_id=1, source_target_pairs={{0,12},{2,14},{4,8},{6,10},{8,4},{10,6},{12,0},{14,2},{1,13},{3,15... | collective-permute-start | bytes 98312 | tf_op jit(solution)/shard_map/ppermute | solution.py:43
  32.9 6.7 %collective-permute-start.15 = (bf16[8,16,128]{2,1,0:T(8,128)(2,1)S(1)}, bf16[8,16,128]{2,1,0:T(8,128)(2,1)S(1)}, u32[]{:S(2)}, u32[]{:S(2)}) collective-permute-start(bf16[8,16,128]{2,1,0:T(8,128)(2,1)S(1)} %get-tuple-element.37), channel_id=1, source_target_pairs={{0,14},{2,12},{4,10},{6,8},{8,6},{10,4},{12,2},{14,0},{1,15},{3,13... | collective-permute-start | bytes 98312 | tf_op jit(solution)/shard_map/ppermute | solution.py:43
  36.4 3.2 %copy-start = (f32[64]{0:T(128)S(1)}, f32[64]{0:T(128)}, u32[]{:S(2)}) copy-start(f32[64]{0:T(128)} %refs_2_.3) | copy-start | bytes 772
  39.6 1.5 %collective-permute-start.16 = (bf16[64,16,128]{2,1,0:T(8,128)(2,1)S(1)}, bf16[64,16,128]{2,1,0:T(8,128)(2,1)S(1)}, u32[]{:S(2)}, u32[]{:S(2)}) collective-permute-start(bf16[64,16,128]{2,1,0:T(8,128)(2,1)S(1)} %constant_dynamic-update-slice_fusion.refs_0_), channel_id=1, source_target_pairs={{1,0},{0,1},{3,2},{2,3},{5,4},{4,5},{7,6},{6,7},{9,8},{8,9},{11,10... | collective-permute-start | bytes 786440 | tf_op jit(solution)/shard_map/ppermute | solution.py:34
  39.6 1.5 %collective-permute-start.17 = (f32[64]{0:T(128)S(1)}, f32[64]{0:T(128)S(1)}, u32[]{:S(2)}, u32[]{:S(2)}) collective-permute-start(f32[64]{0:T(128)S(1)} %copy-done), channel_id=1, source_target_pairs={{1,0},{0,1},{3,2},{2,3},{5,4},{4,5},{7,6},{6,7},{9,8},{8,9},{11,10... | collective-permute-start | bytes 776 | tf_op jit(solution)/shard_map/ppermute | solution.py:34
where the time goes:
time: 43.7 us; the launch traced here: 43.4 us
  starting transfers between devices  24.8 us (57%)
  waiting for transfers between devices  12.6 us (29%)
  Pallas kernels  5.91 us (14%)
    ppermute x14, starting transfers between devices, row_exchange(): lax.ppermute(blocks[d], 'row', [(i, i ^ d) for i in range(count)])  23.8 us
    ppermute x14, waiting for transfers between devices, row_exchange(): lax.ppermute(blocks[d], 'row', [(i, i ^ d) for i in range(count)])  11.2 us
    pallas_call x4, Pallas kernels, call(): pl.pallas_call(body, out_shape=out_shapes, scratch_shapes=scratch, in_spe...  5.91 us
    ppermute x4, waiting for transfers between devices, channel_parts(): lax.ppermute(value, 'ch', [((i + s) % count, i) for i in range(count)])  1.38 us
    ppermute x4, starting transfers between devices, channel_parts(): lax.ppermute(value, 'ch', [((i + s) % count, i) for i in range(count)])  1.01 us
  transfers between devices with their start and end apart: 18, of which 6 were waited for; matrix products, arithmetic and copies ran while one was open for 0% of the time, Pallas kernels for 2%

commit v1 on v0

--- a/solution.py
+++ b/solution.py
@@ -44,17 +44,18 @@
     return arrived
 
 
-def part_start(s, count, size):
-    return pl.multiple_of(((lax.axis_index("ch") + s) % count) * size, size)
-
-
 def fill_gains(gains, gain_scr):
-    count = len(gains)
     size = gains[0].shape[0]
     lanes = gain_scr.shape[1]
-    for s in range(count):
-        line = jnp.broadcast_to(gains[s][...].reshape(1, size), (lanes, size))
-        gain_scr[pl.ds(part_start(s, count, size), size), :] = line.T
+    for s, gain in enumerate(gains):
+        line = jnp.broadcast_to(gain[...].reshape(1, size), (lanes, size))
+        gain_scr[s * size : (s + 1) * size, :] = line.T
+
+
+def own_first(weight):
+    channels = weight.shape[1]
+    own = lax.axis_index("ch") * (channels // lax.axis_size("ch"))
+    return pltpu.roll(weight[...].astype(F32), (channels - own) % channels, 1)
 
 
 def normalise(values, gain):
@@ -64,44 +65,59 @@
     return (centred * lax.rsqrt(spread + EPS) * gain).astype(BF16)
 
 
-def edges_body(count, row_count, *refs):
-    acts, gains = refs[:count], refs[count : 2 * count]
-    lp, lg, rp, rg = refs[2 * count : 2 * count + 4]
-    outs = refs[2 * count + 4 : 2 * count + 4 + row_count]
-    normed_ref, flat, gain_scr, weights = refs[2 * count + 4 + row_count :]
-    size, rows, cols = acts[0].shape
-    channels = size * count
+def prepare_body(row_count, act, lp, lg, rp, rg, flat, stacked, weights):
+    size, rows, cols = act.shape
     hidden = lp.shape[0]
     group = hidden // row_count
     me = lax.axis_index("row")
-    fill_gains(gains, gain_scr)
-    for s in range(count):
-        flat[pl.ds(part_start(s, count, size) * rows, size * rows), :] = (
-            acts[s][...].astype(F32).reshape(size * rows, cols)
-        )
     for n, w in enumerate((lp, rp, lg, rg)):
-        weights[n] = w[...].astype(F32)
+        weights[n] = own_first(w)
     pieces = []
     for pair in ((0, 1), (2, 3)):
         for d in range(row_count):
             start = pl.multiple_of((me ^ d) * group, group)
             for n in pair:
                 pieces.append(weights[n, pl.ds(start, group), :])
-    stacked = jnp.concatenate(pieces, axis=0).astype(BF16)
-    half = 2 * hidden
+    stacked[...] = jnp.concatenate(pieces, axis=0).astype(BF16)
+    flat[...] = act[...].astype(F32).reshape(size * rows, cols)
+
+
+def edges_body(count, row_count, *refs):
+    own, stacked, refs = refs[0], refs[1], refs[2:]
+    others, gains, refs = refs[: count - 1], refs[count - 1 : 2 * count - 1], refs[2 * count - 1 :]
+    outs, refs = refs[:row_count], refs[row_count:]
+    normed_ref, flat, gain_scr = refs
+    rows, pair, cols = outs[0].shape
+    size = own.shape[0] // rows
+    half = stacked.shape[0] // 2
+    fill_gains(gains, gain_scr)
+    for s, other in enumerate(others):
+        flat[s * size * rows : (s + 1) * size * rows, :] = (
+            other[...].astype(F32).reshape(size * rows, cols)
+        )
     gain = gain_scr[...]
     for x in range(rows):
-        normed = normalise(flat[pl.ds(x, channels, stride=rows), :], gain)
+        values = jnp.concatenate(
+            [own[pl.ds(x, size, stride=rows), :]]
+            + [flat[pl.ds(x, (count - 1) * size, stride=rows), :]] * (count > 1),
+            axis=0,
+        )
+        normed = normalise(values, gain)
         normed_ref[x] = normed
-        lifted = jnp.dot(stacked, normed, preferred_element_type=F32)
+        lifted = jnp.dot(stacked[...], normed, preferred_element_type=F32)
         edges = (jax.nn.sigmoid(lifted[half:]) * lifted[:half]).astype(BF16)
         for d in range(row_count):
-            outs[d][x] = edges[2 * group * d : 2 * group * (d + 1)]
-
-
-def gate_body(normed, weight, out):
+            outs[d][x] = edges[pair * d : pair * (d + 1)]
+
+
+def gate_body(count, *refs):
+    normed, gate_weight, proj_weight = refs[:3]
+    gains, (gate, weight, gain_col) = refs[3 : 3 + count], refs[3 + count :]
+    fill_gains(gains, gain_col)
+    weight[...] = own_first(proj_weight).astype(BF16)
+    rotated = own_first(gate_weight).astype(BF16)
     for x in range(normed.shape[0]):
-        out[x] = jax.nn.sigmoid(jnp.dot(weight[...], normed[x], preferred_element_type=F32))
+        gate[x] = jax.nn.sigmoid(jnp.dot(rotated, normed[x], preferred_element_type=F32))
 
 
 def triangle_body(row_count, separate, *refs):
@@ -134,21 +150,19 @@
 
 
 def update_body(count, row_count, *refs):
-    tris, gains = refs[:count], refs[count : 2 * count]
-    gate, weight, out, flat, gain_scr, wide = refs[2 * count :]
+    tris = refs[:count]
+    gate, weight, gain_col, out, flat, wide = refs[count:]
     size, rows, cols = tris[0].shape
     group = size // row_count
     channels = size * count
     me = lax.axis_index("row")
-    fill_gains(gains, gain_scr)
     for s in range(count):
-        base = part_start(s, count, size)
         for d in range(row_count):
-            start = pl.multiple_of((base + (me ^ d) * group) * rows, group * rows)
+            start = pl.multiple_of((s * size + (me ^ d) * group) * rows, group * rows)
             flat[pl.ds(start, group * rows), :] = (
                 tris[s][group * d : group * (d + 1)].astype(F32).reshape(group * rows, cols)
             )
-    gain = gain_scr[...]
+    gain = gain_col[...]
     outs = weight.shape[0]
     for x in range(rows):
         mid = normalise(flat[pl.ds(x, channels, stride=rows), :], gain)
@@ -174,21 +188,35 @@
     acts = channel_parts(pair_act)
     in_gains = channel_parts(in_gain)
     out_gains = channel_parts(out_gain)
+    flat, stacked = call(
+        functools.partial(prepare_body, row_count),
+        [shape((size * rows, cols), F32), shape((4 * hidden, channels), BF16)],
+        [pltpu.VMEM((4, hidden, channels), F32)],
+        1 << 20,
+        pair_act, left_proj.T, left_gate.T, right_proj.T, right_gate.T,
+    )
     *edges, normed = call(
         functools.partial(edges_body, count, row_count),
-        [shape((rows, 2 * group, cols), BF16)] * row_count + [shape((rows, channels, cols), BF16)],
-        [
-            pltpu.VMEM((channels * rows, cols), F32),
+        [shape((rows, 2 * group, cols), BF16)] * row_count
+        + [shape((rows, channels, cols), BF16)],
+        [
+            pltpu.VMEM((max(count - 1, 1) * size * rows, cols), F32),
             pltpu.VMEM((channels, cols), F32),
-            pltpu.VMEM((4, hidden, channels), F32),
         ],
         8 * hidden * channels * rows * cols,
-        *acts, *in_gains, left_proj.T, left_gate.T, right_proj.T, right_gate.T,
+        near(flat), near(stacked), *acts[1:], *in_gains,
     )
     arrived = row_exchange(edges)
-    gate_map = call(
-        gate_body, shape((rows, outs, cols), F32), [], 2 * outs * channels * rows * cols,
-        near(normed), out_gate.T,
+    late = call(
+        functools.partial(gate_body, count),
+        [
+            shape((rows, outs, cols), F32),
+            shape((outs, hidden_all), BF16),
+            shape((hidden_all, cols), F32),
+        ],
+        [],
+        2 * outs * channels * rows * cols,
+        near(normed), out_gate.T, out_proj.T, *out_gains,
     )
     depth = rows * row_count
     separate = col_count > 1
@@ -213,11 +241,10 @@
         jax.ShapeDtypeStruct((outs, rows, cols), BF16),
         [
             pltpu.VMEM((hidden_all * rows, cols), F32),
-            pltpu.VMEM((hidden_all, cols), F32),
             pltpu.VMEM((outs * rows, cols), F32),
         ],
         2 * hidden_all * outs * rows * cols,
-        near(tri), *tris[1:], *out_gains, near(gate_map), out_proj.T,
+        near(tri), *tris[1:], *map(near, late),
     )
 
 

time: 43.7 us -> 43.6 us (level)
    pallas_call x4 -> x5, Pallas kernels: 5.91 us -> 5.95 us  [call(): pl.pallas_call(body, out_shape=out_shapes, scratch_shapes=scratch, in_spe...]
  transfers between devices with their start and end apart: 18 -> 18, of which waited for: 6 -> 7; matrix products, arithmetic and copies ran while one was open for 0% -> 0% of each run, Pallas kernels for 2% -> 5%
where the time goes in v1:
time: 43.6 us; the launch traced here: 43.4 us
  starting transfers between devices  24.8 us (57%)
  waiting for transfers between devices  12.5 us (29%)
  Pallas kernels  5.95 us (14%)
    ppermute x14, starting transfers between devices, row_exchange(): lax.ppermute(blocks[d], 'row', [(i, i ^ d) for i in range(count)])  23.8 us
    ppermute x14, waiting for transfers between devices, row_exchange(): lax.ppermute(blocks[d], 'row', [(i, i ^ d) for i in range(count)])  11.2 us
    pallas_call x5, Pallas kernels, call(): pl.pallas_call(body, out_shape=out_shapes, scratch_shapes=scratch, in_spe...  5.95 us
    ppermute x4, waiting for transfers between devices, channel_parts(): lax.ppermute(value, 'ch', [((i + s) % count, i) for i in range(count)])  1.26 us
    ppermute x4, starting transfers between devices, channel_parts(): lax.ppermute(value, 'ch', [((i + s) % count, i) for i in range(count)])  1.01 us
  transfers between devices with their start and end apart: 18, of which 7 were waited for; matrix products, arithmetic and copies ran while one was open for 0% of the time, Pallas kernels for 5%

profile of v1, /device:TPU:0, one launch (start us, length us, event | category | flops | bytes accessed | tf_op | source)
XLA Modules:
  0.0 43.4 jit_solution(9264202608664459928)
XLA Ops:
  0.0 0.5 %collective-permute-start = (bf16[64,16,128]{2,1,0:T(8,128)(2,1)}, bf16[64,16,128]{2,1,0:T(8,128)(2,1)S(1)}, u32[]{:S(2)}, u32[]{:S(2)}) collective-permute-start(bf16[64,16,128]{2,1,0:T(8,128)(2,1)} %act.1), channel_id=1, source_target_pairs={{1,0},{0,1},{3,2},{2,3},{5,4},{4,5},{7,6},{6,7},{9,8},{8,9},{11,10... | collective-permute-start | bytes 786440 | tf_op jit(solution)/shard_map/ppermute | solution.py:34
  0.5 1.1 %shard_map.91 = (f32[1024,128]{1,0:T(8,128)S(1)}, bf16[256,128]{1,0:T(8,128)(2,1)S(1)}) custom-call(bf16[64,16,128]{2,1,0:T(8,128)(2,1)} %act.1, bf16[64,128]{1,0:T(8,128)(2,1)} %bitcast.6, bf16[64,128]{1,0:T(8,128)(2,1)} %bitcast.7, bf16[64,128]{1,0:T(8,128)(2,1)} %bitcast.8, bf16[64,128]{1,0:T(8,128)(2,1)} %bitcast.9), custom_call_target="tpu_custom_call" | custom-call | flops 1048576 | bytes 1048576 | tf_op jit(solution)/shard_map/pallas_call | solution.py:21
  1.6 0.2 collective-permute-done.1.refs_4_
  1.9 1.6 %shard_map.92 = (bf16[16,16,128]{2,1,0:T(8,128)(2,1)S(1)}, bf16[16,16,128]{2,1,0:T(8,128)(2,1)S(1)}, bf16[16,16,128]{2,1,0:T(8,128)(2,1)S(1)}, bf16[16,16,128]{2...) custom-call(f32[1024,128]{1,0:T(8,128)S(1)} %get-tuple-element.27.re, ...), custom_call_target="tpu_custom_call" | custom-call | flops 134217728 | bytes 1048576 | tf_op jit(solution)/shard_map/pallas_call | solution.py:21
  3.5 2.9 %collective-permute-start.2 = (bf16[16,16,128]{2,1,0:T(8,128)(2,1)S(1)}, bf16[16,16,128]{2,1,0:T(8,128)(2,1)S(1)}, u32[]{:S(2)}, u32[]{:S(2)}) collective-permute-start(bf16[16,16,128]{2,1,0:T(8,128)(2,1)S(1)} %get-tuple-element.30), channel_id=1, source_target_pairs={{0,2},{2,0},{4,6},{6,4},{8,10},{10,8},{12,14},{14,12},{1,3},{3,1},... | collective-permute-start | bytes 196616 | tf_op jit(solution)/shard_map/ppermute | solution.py:43
  6.4 1.6 %collective-permute-start.3 = (bf16[16,16,128]{2,1,0:T(8,128)(2,1)S(1)}, bf16[16,16,128]{2,1,0:T(8,128)(2,1)S(1)}, u32[]{:S(2)}, u32[]{:S(2)}) collective-permute-start(bf16[16,16,128]{2,1,0:T(8,128)(2,1)S(1)} %get-tuple-element.31), channel_id=1, source_target_pairs={{0,4},{2,6},{4,0},{6,2},{8,12},{10,14},{12,8},{14,10},{1,5},{3,7},... | collective-permute-start | bytes 196616 | tf_op jit(solution)/shard_map/ppermute | solution.py:43
  8.0 3.0 %collective-permute-start.5 = (bf16[16,16,128]{2,1,0:T(8,128)(2,1)S(1)}, bf16[16,16,128]{2,1,0:T(8,128)(2,1)S(1)}, u32[]{:S(2)}, u32[]{:S(2)}) collective-permute-start(bf16[16,16,128]{2,1,0:T(8,128)(2,1)S(1)} %get-tuple-element.33), channel_id=1, source_target_pairs={{0,8},{2,10},{4,12},{6,14},{8,0},{10,2},{12,4},{14,6},{1,9},{3,11}... | collective-permute-start | bytes 196616 | tf_op jit(solution)/shard_map/ppermute | solution.py:43
  11.0 1.3 %collective-permute-start.6 = (bf16[16,16,128]{2,1,0:T(8,128)(2,1)S(1)}, bf16[16,16,128]{2,1,0:T(8,128)(2,1)S(1)}, u32[]{:S(2)}, u32[]{:S(2)}) collective-permute-start(bf16[16,16,128]{2,1,0:T(8,128)(2,1)S(1)} %get-tuple-element.34), channel_id=1, source_target_pairs={{0,10},{2,8},{4,14},{6,12},{8,2},{10,0},{12,6},{14,4},{1,11},{3,9}... | collective-permute-start | bytes 196616 | tf_op jit(solution)/shard_map/ppermute | solution.py:43
  12.2 3.6 %collective-permute-start.7 = (bf16[16,16,128]{2,1,0:T(8,128)(2,1)S(1)}, bf16[16,16,128]{2,1,0:T(8,128)(2,1)S(1)}, u32[]{:S(2)}, u32[]{:S(2)}) collective-permute-start(bf16[16,16,128]{2,1,0:T(8,128)(2,1)S(1)} %get-tuple-element.35), channel_id=1, source_target_pairs={{0,12},{2,14},{4,8},{6,10},{8,4},{10,6},{12,0},{14,2},{1,13},{3,15... | collective-permute-start | bytes 196616 | tf_op jit(solution)/shard_map/ppermute | solution.py:43
  15.9 5.5 %collective-permute-done.6.refs_5_ = bf16[16,16,128]{2,1,0:T(8,128)(2,1)S(1)} collective-permute-done((bf16[16,16,128]{2,1,0:T(8,128)(2,1)S(1)}, bf16[16,16,128]{2,1,0:T(8,128)(2,1)S(1)}, u32[]{:S(2)}, u32[]{:S(2)}) %collective-permute-start.6) | collective-permute-done | bytes 65568 | tf_op jit(solution)/shard_map/ppermute | solution.py:43
  21.4 1.5 %collective-permute-done.8.refs_7_ = bf16[16,16,128]{2,1,0:T(8,128)(2,1)S(1)} collective-permute-done((bf16[16,16,128]{2,1,0:T(8,128)(2,1)S(1)}, bf16[16,16,128]{2,1,0:T(8,128)(2,1)S(1)}, u32[]{:S(2)}, u32[]{:S(2)}) %collective-permute-start.8) | collective-permute-done | bytes 65568 | tf_op jit(solution)/shard_map/ppermute | solution.py:43
  22.9 0.5 %shard_map.93 = (bf16[8,16,128]{2,1,0:T(8,128)(2,1)S(1)}, bf16[8,16,128]{2,1,0:T(8,128)(2,1)S(1)}, bf16[8,16,128]{2,1,0:T(8,128)(2,1)S(1)}, bf16[8,16,128]{2,1,0...) custom-call(bf16[16,16,128]{2,1,0:T(8,128)(2,1)S(1)} %get-tuple-elem, ...), custom_call_target="tpu_custom_call" | custom-call | flops 33554432 | bytes 1048576 | tf_op jit(solution)/shard_map/pallas_call | solution.py:21
  23.5 0.6 %collective-permute-start.9 = (bf16[8,16,128]{2,1,0:T(8,128)(2,1)S(1)}, bf16[8,16,128]{2,1,0:T(8,128)(2,1)S(1)}, u32[]{:S(2)}, u32[]{:S(2)}) collective-permute-start(bf16[8,16,128]{2,1,0:T(8,128)(2,1)S(1)} %get-tuple-element.38), channel_id=1, source_target_pairs={{0,2},{2,0},{4,6},{6,4},{8,10},{10,8},{12,14},{14,12},{1,3},{3,1},... | collective-permute-start | bytes 98312 | tf_op jit(solution)/shard_map/ppermute | solution.py:43
  24.1 2.2 %collective-permute-start.10 = (bf16[8,16,128]{2,1,0:T(8,128)(2,1)S(1)}, bf16[8,16,128]{2,1,0:T(8,128)(2,1)S(1)}, u32[]{:S(2)}, u32[]{:S(2)}) collective-permute-start(bf16[8,16,128]{2,1,0:T(8,128)(2,1)S(1)} %get-tuple-element.39), channel_id=1, source_target_pairs={{0,4},{2,6},{4,0},{6,2},{8,12},{10,14},{12,8},{14,10},{1,5},{3,7},... | collective-permute-start | bytes 98312 | tf_op jit(solution)/shard_map/ppermute | solution.py:43
  26.3 0.7 %collective-permute-start.11 = (bf16[8,16,128]{2,1,0:T(8,128)(2,1)S(1)}, bf16[8,16,128]{2,1,0:T(8,128)(2,1)S(1)}, u32[]{:S(2)}, u32[]{:S(2)}) collective-permute-start(bf16[8,16,128]{2,1,0:T(8,128)(2,1)S(1)} %get-tuple-element.40), channel_id=1, source_target_pairs={{0,6},{2,4},{4,2},{6,0},{8,14},{10,12},{12,10},{14,8},{1,7},{3,5},... | collective-permute-start | bytes 98312 | tf_op jit(solution)/shard_map/ppermute | solution.py:43
  27.0 3.0 %collective-permute-start.12 = (bf16[8,16,128]{2,1,0:T(8,128)(2,1)S(1)}, bf16[8,16,128]{2,1,0:T(8,128)(2,1)S(1)}, u32[]{:S(2)}, u32[]{:S(2)}) collective-permute-start(bf16[8,16,128]{2,1,0:T(8,128)(2,1)S(1)} %get-tuple-element.41), channel_id=1, source_target_pairs={{0,8},{2,10},{4,12},{6,14},{8,0},{10,2},{12,4},{14,6},{1,9},{3,11}... | collective-permute-start | bytes 98312 | tf_op jit(solution)/shard_map/ppermute | solution.py:43
  30.1 2.3 %collective-permute-start.14 = (bf16[8,16,128]{2,1,0:T(8,128)(2,1)S(1)}, bf16[8,16,128]{2,1,0:T(8,128)(2,1)S(1)}, u32[]{:S(2)}, u32[]{:S(2)}) collective-permute-start(bf16[8,16,128]{2,1,0:T(8,128)(2,1)S(1)} %get-tuple-element.43), channel_id=1, source_target_pairs={{0,12},{2,14},{4,8},{6,10},{8,4},{10,6},{12,0},{14,2},{1,13},{3,15... | collective-permute-start | bytes 98312 | tf_op jit(solution)/shard_map/ppermute | solution.py:43
  32.4 2.4 %collective-permute-start.15 = (bf16[8,16,128]{2,1,0:T(8,128)(2,1)S(1)}, bf16[8,16,128]{2,1,0:T(8,128)(2,1)S(1)}, u32[]{:S(2)}, u32[]{:S(2)}) collective-permute-start(bf16[8,16,128]{2,1,0:T(8,128)(2,1)S(1)} %get-tuple-element.44), channel_id=1, source_target_pairs={{0,14},{2,12},{4,10},{6,8},{8,6},{10,4},{12,2},{14,0},{1,15},{3,13... | collective-permute-start | bytes 98312 | tf_op jit(solution)/shard_map/ppermute | solution.py:43
  34.9 0.9 %collective-permute-done.13 = bf16[8,16,128]{2,1,0:T(8,128)(2,1)S(1)} collective-permute-done((bf16[8,16,128]{2,1,0:T(8,128)(2,1)S(1)}, bf16[8,16,128]{2,1,0:T(8,128)(2,1)S(1)}, u32[]{:S(2)}, u32[]{:S(2)}) %collective-permute-start.13) | collective-permute-done | bytes 32800 | tf_op jit(solution)/shard_map/ppermute | solution.py:43
  35.9 3.2 %collective-permute-done.15 = bf16[8,16,128]{2,1,0:T(8,128)(2,1)S(1)} collective-permute-done((bf16[8,16,128]{2,1,0:T(8,128)(2,1)S(1)}, bf16[8,16,128]{2,1,0:T(8,128)(2,1)S(1)}, u32[]{:S(2)}, u32[]{:S(2)}) %collective-permute-start.15) | collective-permute-done | bytes 32800 | tf_op jit(solution)/shard_map/ppermute | solution.py:43
  39.1 0.5 %collective-permute-start.17 = (f32[64]{0:T(128)S(1)}, f32[64]{0:T(128)S(1)}, u32[]{:S(2)}, u32[]{:S(2)}) collective-permute-start(f32[64]{0:T(128)S(1)} %copy-done), channel_id=1, source_target_pairs={{1,0},{0,1},{3,2},{2,3},{5,4},{4,5},{7,6},{6,7},{9,8},{8,9},{11,10... | collective-permute-start | bytes 776 | tf_op jit(solution)/shard_map/ppermute | solution.py:34
  39.6 1.0 %collective-permute-done.17.refs_4_ = f32[64]{0:T(128)S(1)} collective-permute-done((f32[64]{0:T(128)S(1)}, f32[64]{0:T(128)S(1)}, u32[]{:S(2)}, u32[]{:S(2)}) %collective-permute-start.17) | collective-permute-done | bytes 288 | tf_op jit(solution)/shard_map/ppermute | solution.py:34
  40.7 1.1 %shard_map.94 = (f32[16,64,128]{2,1,0:T(8,128)S(1)}, bf16[64,128]{1,0:T(8,128)(2,1)S(1)}, f32[128,128]{1,0:T(8,128)S(1)}) custom-call(bf16[16,128,128]{2,1,0:T(8,128)(2,1)S(1)} %get-tuple-element.45.refs_0_, bf16[64,128]{1,0:T(8,128)(2,1)} %bitcast.10, bf16[64,128]{1,0:T(8,128)(2,1)} %bitcast.11, f32[64]{0:T(128)} %refs_3_.3, ...), custom_call_target="tpu_custom_call" | custom-call | flops 33554432 | bytes 1048576 | tf_op jit(solution)/shard_map/pallas_call | solution.py:21
  41.8 1.6 %shard_map.95 = bf16[64,16,128]{2,1,0:T(8,128)(2,1)} custom-call(bf16[64,16,128]{2,1,0:T(8,128)(2,1)S(1)} %constant_dynamic-update-slice_fusion.refs_0_, bf16[64,16,128]{2,1,0:T(8,128)(2,1)S(1)} %collective-permute-done.16.refs_1_, f32[16,64,128]{2,1,0:T(8,128)S(1)} %get-tuple-element.46.refs_2_, bf16[64,128]{1,0:T(8,128)(2,1)S(1)} %get-tuple-element.47.refs_3_, ...), custom_call_target="tpu_custom_call" | custom-call | flops 33554432 | bytes 1048576 | tf_op jit(solution)/shard_map/pallas_call | solution.py:21
  (27 shorter events, 0.4 us)
Async XLA Ops:
  0.0 1.9 %collective-permute-start = (bf16[64,16,128]{2,1,0:T(8,128)(2,1)}, bf16[64,16,128]{2,1,0:T(8,128)(2,1)S(1)}, u32[]{:S(2)}, u32[]{:S(2)}) collective-permute-start(bf16[64,16,128]{2,1,0:T(8,128)(2,1)} %act.1), channel_id=1, source_target_pairs={{1,0},{0,1},{3,2},{2,3},{5,4},{4,5},{7,6},{6,7},{9,8},{8,9},{11,10... | collective-permute-start | bytes 786440 | tf_op jit(solution)/shard_map/ppermute | solution.py:34
  0.5 1.4 %collective-permute-start.1 = (f32[64]{0:T(128)}, f32[64]{0:T(128)S(1)}, u32[]{:S(2)}, u32[]{:S(2)}) collective-permute-start(f32[64]{0:T(128)} %refs_3_.2), channel_id=1, source_target_pairs={{1,0},{0,1},{3,2},{2,3},{5,4},{4,5},{7,6},{6,7},{9,8},{8,9},{11,10... | collective-permute-start | bytes 776 | tf_op jit(solution)/shard_map/ppermute | solution.py:34
  3.5 8.8 %collective-permute-start.2 = (bf16[16,16,128]{2,1,0:T(8,128)(2,1)S(1)}, bf16[16,16,128]{2,1,0:T(8,128)(2,1)S(1)}, u32[]{:S(2)}, u32[]{:S(2)}) collective-permute-start(bf16[16,16,128]{2,1,0:T(8,128)(2,1)S(1)} %get-tuple-element.30), channel_id=1, source_target_pairs={{0,2},{2,0},{4,6},{6,4},{8,10},{10,8},{12,14},{14,12},{1,3},{3,1},... | collective-permute-start | bytes 196616 | tf_op jit(solution)/shard_map/ppermute | solution.py:43
  6.4 9.5 %collective-permute-start.3 = (bf16[16,16,128]{2,1,0:T(8,128)(2,1)S(1)}, bf16[16,16,128]{2,1,0:T(8,128)(2,1)S(1)}, u32[]{:S(2)}, u32[]{:S(2)}) collective-permute-start(bf16[16,16,128]{2,1,0:T(8,128)(2,1)S(1)} %get-tuple-element.31), channel_id=1, source_target_pairs={{0,4},{2,6},{4,0},{6,2},{8,12},{10,14},{12,8},{14,10},{1,5},{3,7},... | collective-permute-start | bytes 196616 | tf_op jit(solution)/shard_map/ppermute | solution.py:43
  8.0 7.9 %collective-permute-start.4 = (bf16[16,16,128]{2,1,0:T(8,128)(2,1)S(1)}, bf16[16,16,128]{2,1,0:T(8,128)(2,1)S(1)}, u32[]{:S(2)}, u32[]{:S(2)}) collective-permute-start(bf16[16,16,128]{2,1,0:T(8,128)(2,1)S(1)} %get-tuple-element.32), channel_id=1, source_target_pairs={{0,6},{2,4},{4,2},{6,0},{8,14},{10,12},{12,10},{14,8},{1,7},{3,5},... | collective-permute-start | bytes 196616 | tf_op jit(solution)/shard_map/ppermute | solution.py:43
  8.0 7.9 %collective-permute-start.5 = (bf16[16,16,128]{2,1,0:T(8,128)(2,1)S(1)}, bf16[16,16,128]{2,1,0:T(8,128)(2,1)S(1)}, u32[]{:S(2)}, u32[]{:S(2)}) collective-permute-start(bf16[16,16,128]{2,1,0:T(8,128)(2,1)S(1)} %get-tuple-element.33), channel_id=1, source_target_pairs={{0,8},{2,10},{4,12},{6,14},{8,0},{10,2},{12,4},{14,6},{1,9},{3,11}... | collective-permute-start | bytes 196616 | tf_op jit(solution)/shard_map/ppermute | solution.py:43
  11.0 10.5 %collective-permute-start.6 = (bf16[16,16,128]{2,1,0:T(8,128)(2,1)S(1)}, bf16[16,16,128]{2,1,0:T(8,128)(2,1)S(1)}, u32[]{:S(2)}, u32[]{:S(2)}) collective-permute-start(bf16[16,16,128]{2,1,0:T(8,128)(2,1)S(1)} %get-tuple-element.34), channel_id=1, source_target_pairs={{0,10},{2,8},{4,14},{6,12},{8,2},{10,0},{12,6},{14,4},{1,11},{3,9}... | collective-permute-start | bytes 196616 | tf_op jit(solution)/shard_map/ppermute | solution.py:43
  12.2 9.2 %collective-permute-start.7 = (bf16[16,16,128]{2,1,0:T(8,128)(2,1)S(1)}, bf16[16,16,128]{2,1,0:T(8,128)(2,1)S(1)}, u32[]{:S(2)}, u32[]{:S(2)}) collective-permute-start(bf16[16,16,128]{2,1,0:T(8,128)(2,1)S(1)} %get-tuple-element.35), channel_id=1, source_target_pairs={{0,12},{2,14},{4,8},{6,10},{8,4},{10,6},{12,0},{14,2},{1,13},{3,15... | collective-permute-start | bytes 196616 | tf_op jit(solution)/shard_map/ppermute | solution.py:43
  15.8 7.1 %collective-permute-start.8 = (bf16[16,16,128]{2,1,0:T(8,128)(2,1)S(1)}, bf16[16,16,128]{2,1,0:T(8,128)(2,1)S(1)}, u32[]{:S(2)}, u32[]{:S(2)}) collective-permute-start(bf16[16,16,128]{2,1,0:T(8,128)(2,1)S(1)} %get-tuple-element.36), channel_id=1, source_target_pairs={{0,14},{2,12},{4,10},{6,8},{8,6},{10,4},{12,2},{14,0},{1,15},{3,13... | collective-permute-start | bytes 196616 | tf_op jit(solution)/shard_map/ppermute | solution.py:43
  23.5 6.7 %collective-permute-start.9 = (bf16[8,16,128]{2,1,0:T(8,128)(2,1)S(1)}, bf16[8,16,128]{2,1,0:T(8,128)(2,1)S(1)}, u32[]{:S(2)}, u32[]{:S(2)}) collective-permute-start(bf16[8,16,128]{2,1,0:T(8,128)(2,1)S(1)} %get-tuple-element.38), channel_id=1, source_target_pairs={{0,2},{2,0},{4,6},{6,4},{8,10},{10,8},{12,14},{14,12},{1,3},{3,1},... | collective-permute-start | bytes 98312 | tf_op jit(solution)/shard_map/ppermute | solution.py:43
  24.1 8.4 %collective-permute-start.10 = (bf16[8,16,128]{2,1,0:T(8,128)(2,1)S(1)}, bf16[8,16,128]{2,1,0:T(8,128)(2,1)S(1)}, u32[]{:S(2)}, u32[]{:S(2)}) collective-permute-start(bf16[8,16,128]{2,1,0:T(8,128)(2,1)S(1)} %get-tuple-element.39), channel_id=1, source_target_pairs={{0,4},{2,6},{4,0},{6,2},{8,12},{10,14},{12,8},{14,10},{1,5},{3,7},... | collective-permute-start | bytes 98312 | tf_op jit(solution)/shard_map/ppermute | solution.py:43
  26.3 8.6 %collective-permute-start.11 = (bf16[8,16,128]{2,1,0:T(8,128)(2,1)S(1)}, bf16[8,16,128]{2,1,0:T(8,128)(2,1)S(1)}, u32[]{:S(2)}, u32[]{:S(2)}) collective-permute-start(bf16[8,16,128]{2,1,0:T(8,128)(2,1)S(1)} %get-tuple-element.40), channel_id=1, source_target_pairs={{0,6},{2,4},{4,2},{6,0},{8,14},{10,12},{12,10},{14,8},{1,7},{3,5},... | collective-permute-start | bytes 98312 | tf_op jit(solution)/shard_map/ppermute | solution.py:43
  27.0 7.9 %collective-permute-start.12 = (bf16[8,16,128]{2,1,0:T(8,128)(2,1)S(1)}, bf16[8,16,128]{2,1,0:T(8,128)(2,1)S(1)}, u32[]{:S(2)}, u32[]{:S(2)}) collective-permute-start(bf16[8,16,128]{2,1,0:T(8,128)(2,1)S(1)} %get-tuple-element.41), channel_id=1, source_target_pairs={{0,8},{2,10},{4,12},{6,14},{8,0},{10,2},{12,4},{14,6},{1,9},{3,11}... | collective-permute-start | bytes 98312 | tf_op jit(solution)/shard_map/ppermute | solution.py:43
  30.0 5.7 %collective-permute-start.13 = (bf16[8,16,128]{2,1,0:T(8,128)(2,1)S(1)}, bf16[8,16,128]{2,1,0:T(8,128)(2,1)S(1)}, u32[]{:S(2)}, u32[]{:S(2)}) collective-permute-start(bf16[8,16,128]{2,1,0:T(8,128)(2,1)S(1)} %get-tuple-element.42), channel_id=1, source_target_pairs={{0,10},{2,8},{4,14},{6,12},{8,2},{10,0},{12,6},{14,4},{1,11},{3,9}... | collective-permute-start | bytes 98312 | tf_op jit(solution)/shard_map/ppermute | solution.py:43
  30.1 5.8 %collective-permute-start.14 = (bf16[8,16,128]{2,1,0:T(8,128)(2,1)S(1)}, bf16[8,16,128]{2,1,0:T(8,128)(2,1)S(1)}, u32[]{:S(2)}, u32[]{:S(2)}) collective-permute-start(bf16[8,16,128]{2,1,0:T(8,128)(2,1)S(1)} %get-tuple-element.43), channel_id=1, source_target_pairs={{0,12},{2,14},{4,8},{6,10},{8,4},{10,6},{12,0},{14,2},{1,13},{3,15... | collective-permute-start | bytes 98312 | tf_op jit(solution)/shard_map/ppermute | solution.py:43
  32.4 6.7 %collective-permute-start.15 = (bf16[8,16,128]{2,1,0:T(8,128)(2,1)S(1)}, bf16[8,16,128]{2,1,0:T(8,128)(2,1)S(1)}, u32[]{:S(2)}, u32[]{:S(2)}) collective-permute-start(bf16[8,16,128]{2,1,0:T(8,128)(2,1)S(1)} %get-tuple-element.44), channel_id=1, source_target_pairs={{0,14},{2,12},{4,10},{6,8},{8,6},{10,4},{12,2},{14,0},{1,15},{3,13... | collective-permute-start | bytes 98312 | tf_op jit(solution)/shard_map/ppermute | solution.py:43
  35.9 3.2 %copy-start = (f32[64]{0:T(128)S(1)}, f32[64]{0:T(128)}, u32[]{:S(2)}) copy-start(f32[64]{0:T(128)} %refs_3_.3) | copy-start | bytes 772
  39.1 2.6 %collective-permute-start.16 = (bf16[64,16,128]{2,1,0:T(8,128)(2,1)S(1)}, bf16[64,16,128]{2,1,0:T(8,128)(2,1)S(1)}, u32[]{:S(2)}, u32[]{:S(2)}) collective-permute-start(bf16[64,16,128]{2,1,0:T(8,128)(2,1)S(1)} %constant_dynamic-update-slice_fusion.refs_0_), channel_id=1, source_target_pairs={{1,0},{0,1},{3,2},{2,3},{5,4},{4,5},{7,6},{6,7},{9,8},{8,9},{11,10... | collective-permute-start | bytes 786440 | tf_op jit(solution)/shard_map/ppermute | solution.py:34
  39.1 1.5 %collective-permute-start.17 = (f32[64]{0:T(128)S(1)}, f32[64]{0:T(128)S(1)}, u32[]{:S(2)}, u32[]{:S(2)}) collective-permute-start(f32[64]{0:T(128)S(1)} %copy-done), channel_id=1, source_target_pairs={{1,0},{0,1},{3,2},{2,3},{5,4},{4,5},{7,6},{6,7},{9,8},{8,9},{11,10... | collective-permute-start | bytes 776 | tf_op jit(solution)/shard_map/ppermute | solution.py:34
